TPU v7x, 128 devices: a whole 4x4x4 slice. The times are simulated.
128 devices in a mesh: row: 4 (over z), col: 32 (over x, y, core).
Axes of the slice: x: 4, y: 4, z: 4, core: 2. Of those that a mesh axis runs over, the one named last changes fastest.
Arguments:
- neighbor: int32 [32, 3072, 3072], P(None, 'col', 'row'), may hold values from 0 to 1, as said below
- true_coords: float32 [32, 3, 3072], P(None, None, ('row', 'col')), as said below
- pred_coords: float32 [32, 3, 3072], P(None, None, ('row', 'col')), as said below
- residue_mask: int32 [32, 3072], P(None, ('row', 'col')), may hold values from 0 to 1, as said below
- single: bfloat16 [32, 3072, 384], P(None, ('row', 'col'))
- ln_gain: float32 [384], replicated, may hold values from 0.1 to 1.9
- w_hidden: bfloat16 [384, 128], replicated, may hold values from -0.3125 to 0.3125
- b_hidden: float32 [128], replicated, may hold values from -3 to 3
- w_mid: bfloat16 [128, 128], replicated, may hold values from -0.5 to 0.5
- b_mid: float32 [128], replicated, may hold values from -3 to 3
- w_logits: bfloat16 [128, 50], replicated, may hold values from -1.5 to 1.5
- b_logits: float32 [50], replicated, may hold values from -4 to 4
Outputs:
- lddt_score: float32 [32, 3072], P(None, ('row', 'col'))
- residue_loss: float32 [32, 3072], P(None, ('row', 'col'))
- total_loss: float32 [], replicated
Inputs may be any that keep to these rules, and one draw needn't show every extreme that they name: `neighbor`: 0 or 1; 0 where j == i; 1 wherever 0 < |i - j| <= 8. `residue_mask`: per structure, 1 on a leading run of 1536 or more residues and 0 after it. `true_coords`: positions in angstroms. `pred_coords`: positions in angstroms.
All inputs are finite; a program needn't handle non-finite values.
Results may differ from a plain program's by a relative error of at most 0.00098.
Values sent between devices are 32-bit elements; how exact they have to be, the bound alone decides.
A program may use at most 64 MiB of HBM per device.

v0:
```python
import jax
import jax.numpy as jnp
from jax import lax
from jax.sharding import Mesh
from jax.sharding import PartitionSpec as P

L = 3072
COL = ("col_0", "col_1", "col_2")
ROW_COL = ("row", "col_0", "col_1", "col_2")


THRESHOLDS = (0.5, 1.0, 2.0, 4.0)


def in_order(parts, dim):
    parts = jnp.moveaxis(parts, 0, dim)
    lengths = parts.shape
    return parts.reshape(*lengths[:dim], lengths[dim] * lengths[dim + 1], *lengths[dim + 2 :])


def sent_to_all(shard, axis):
    copies = jnp.broadcast_to(shard, (lax.axis_size(axis), *shard.shape))
    return lax.all_to_all(copies, axis, split_axis=0, concat_axis=0, tiled=True)


def gather_directly(shard, axis, dim):
    return in_order(sent_to_all(shard, axis), dim)


def from_root(shard, axis, root):
    return lax.dynamic_index_in_dim(lax.all_gather(shard, axis), root, 0, keepdims=False)


def split_up(shard, dim, size):
    before, after = (shard.shape[:dim], shard.shape[dim + 1 :])
    return jnp.moveaxis(shard.reshape(*before, size, -1, *after), dim, 0)


def summed_on_arrival(shard, axis, dim):
    size = lax.axis_size(axis)
    parts = lax.all_to_all(split_up(shard, dim, size), axis, 0, 0, tiled=True)
    return jnp.sum(parts, axis=0)


def sent_together(arrays, axis, dim, along):
    ends, at = ([], 0)
    for a in arrays[:-1]:
        at += a.shape[along]
        ends.append(at)
    both = jnp.concatenate(arrays, axis=along)
    return tuple(jnp.split(summed_on_arrival(both, axis, dim), ends, axis=along))


def over_axes(shard, axes):
    for axis in axes:
        shard = lax.psum(shard, axis)
    return shard


def tile_dist(rows_block, cols_block):
    total = (cols_block[:, 0, :, None] - rows_block[:, 0, None, :]) ** 2
    total = total + (cols_block[:, 1, :, None] - rows_block[:, 1, None, :]) ** 2
    total = total + (cols_block[:, 2, :, None] - rows_block[:, 2, None, :]) ** 2
    return jnp.sqrt(total + 1e-10)


def head_loss(lddt_value, single, ln_gain, w_hidden, b_hidden, w_mid, b_mid, w_logits, b_logits):
    features = single.astype(jnp.float32)
    average = jnp.mean(features, axis=-1, keepdims=True)
    centred = features - average
    variance = jnp.mean(centred * centred, axis=-1, keepdims=True)
    normed = (centred * lax.rsqrt(variance + 1e-05) * ln_gain).astype(jnp.bfloat16)
    first_hidden = jax.nn.relu(
        jnp.dot(normed, w_hidden, preferred_element_type=jnp.float32) + b_hidden
    ).astype(jnp.bfloat16)
    second_hidden = jax.nn.relu(
        jnp.dot(first_hidden, w_mid, preferred_element_type=jnp.float32) + b_mid
    ).astype(jnp.bfloat16)
    logits = jnp.dot(second_hidden, w_logits, preferred_element_type=jnp.float32) + b_logits
    log_total = jnp.log(jnp.sum(jnp.exp(logits), axis=-1))
    bins = logits.shape[-1]
    centers = (jnp.arange(bins).astype(jnp.float32) + 0.5) / bins
    closeness = jnp.exp(-((lddt_value[..., None] - centers) ** 2) * (bins * bins * 0.5))
    target = closeness / jnp.sum(closeness, axis=-1, keepdims=True)
    return log_total - jnp.sum(target * logits, axis=-1)


def local(
    neighbor,
    true_coords,
    pred_coords,
    residue_mask,
    single,
    ln_gain,
    w_hidden,
    b_hidden,
    w_mid,
    b_mid,
    w_logits,
    b_logits,
):
    valid = residue_mask.astype(jnp.float32)
    stacked = jnp.concatenate([true_coords, pred_coords, valid[:, None, :]], axis=1)
    row_count = lax.axis_size("row")
    col_count = lax.axis_size(COL)
    rows_len = L // row_count
    cols_len = L // col_count
    col_index = lax.axis_index(COL)
    rows_part = gather_directly(stacked, COL, 2)
    offset = col_index * cols_len % rows_len
    column_piece = lax.dynamic_slice_in_dim(rows_part, offset, cols_len, 2)
    source_row = col_index * cols_len // rows_len
    cols_part = from_root(column_piece, "row", source_row)
    true_dist = tile_dist(rows_part[:, 0:3], cols_part[:, 0:3])
    pred_dist = tile_dist(rows_part[:, 3:6], cols_part[:, 3:6])
    mismatch = jnp.abs(pred_dist - true_dist)
    scores = jnp.zeros_like(mismatch)
    for threshold in THRESHOLDS:
        scores = scores + jax.nn.sigmoid(4.0 * (threshold - mismatch))
    scores = 0.25 * scores
    weights = neighbor.astype(jnp.float32) * rows_part[:, 6, None, :] * cols_part[:, 6, :, None]
    preserved = jnp.sum(weights * scores, axis=1)
    neighbors = jnp.sum(weights, axis=1)
    preserved_own, neighbors_own = sent_together((preserved, neighbors), COL, 1, 0)
    lddt_score = preserved_own / jnp.maximum(neighbors_own, 1.0)
    residue_loss = valid * head_loss(
        lddt_score, single, ln_gain, w_hidden, b_hidden, w_mid, b_mid, w_logits, b_logits
    )
    loss_sum, valid_sum = (
        over_axes(jnp.sum(residue_loss), ROW_COL),
        over_axes(jnp.sum(valid), ROW_COL),
    )
    total_loss = loss_sum / valid_sum
    return (lddt_score, residue_loss, total_loss)


def solution(mesh):
    torus = Mesh(
        mesh.devices.reshape(mesh.shape["row"], 4, 4, 2), ("row", "col_0", "col_1", "col_2")
    )
    placed = (
        P(None, COL, "row"),
        P(None, None, ROW_COL),
        P(None, None, ROW_COL),
        P(None, ROW_COL),
        P(None, ROW_COL, None),
        P(),
        P(),
        P(),
        P(),
        P(),
        P(),
        P(),
    )
    return jax.shard_map(
        local,
        mesh=torus,
        in_specs=placed,
        out_specs=(P(None, ROW_COL), P(None, ROW_COL), P()),
        check_vma=False,
    )
```

profile of v0, /device:TPU:1, one launch (start us, length us, event | category | flops | bytes accessed | tf_op | source)
XLA Modules:
  0.0 134.1 jit_solution(17454920612350802530)
XLA Ops:
  0.6 0.0 copy-start
  0.6 0.8 copy.19
  1.5 0.1 copy.20
  1.5 0.8 pad_maximum_fusion.1
  2.3 0.2 broadcast_bitcast_fusion
  2.5 2.1 %reshape.49 = f32[32,1,5376]{2,1,0:T(1,128)} reshape(f32[32,7,24,32]{3,2,1,0:T(8,128)S(1)} %broadcast_bitcast_fusion) | data formatting | bytes 1376256
  4.6 8.6 %all-to-all-start = ((f32[32,1,5376]{2,1,0:T(1,128)}), f32[32,1,5376]{2,1,0:T(1,128)S(1)}, u32[]{:S(2)}, u32[]{:S(2)}) async-start(f32[32,1,5376]{2,1,0:T(1,128)} %reshape.49), calls=%async_computation | async-start | bytes 1376256 | tf_op jit(solution)/shard_map/all_to_all | solution.py:23
  13.2 1.2 convert_reduce_fusion
  14.4 0.5 add_multiply_fusion
  15.0 1.4 %fusion.8 = f32[32,24]{1,0:T(8,128)S(1)} fusion(bf16[32,24,384]{2,1,0:T(8,128)(2,1)} %param.16, f32[32,24]{1,0:T(8,128)S(1)} %broadcast_multiply_fusion), kind=kLoop, calls=%fused_computation.15 | loop fusion | flops 1178880 | bytes 595968 | tf_op jit(solution)/shard_map/reduce_sum | solution.py:71
  16.4 0.0 copy-done
  16.4 2.6 %fusion.12 = bf16[32,24,128]{2,1,0:T(8,128)(2,1)} fusion(bf16[32,24,384]{2,1,0:T(8,128)(2,1)} %param.16, f32[384]{0:T(512)} %param.17, f32[32,24]{1,0:T(8,128)S(1)} %add_rsqrt_fusion, f32[32,24]{1,0:T(8,128)S(1)} %broadcast_multiply_fusion, f32[128]{0:T(128)} %param.21, f32[128]{0:T(128)} %param.19, bf16[384,128]{1,0:T(8,128)(2,1)S(1)} %copy-done, ...), kind=kOutput, calls=%fused_computation.19 | convolution fusion | flops 102727680 | bytes 926208 | tf_op jit(solution)/shard_map/dot_general | solution.py:77
  19.0 7.5 %all-to-all-done = f32[32,1,5376]{2,1,0:T(1,128)S(1)} async-done(((f32[32,1,5376]{2,1,0:T(1,128)}), f32[32,1,5376]{2,1,0:T(1,128)S(1)}, u32[]{:S(2)}, u32[]{:S(2)}) %all-to-all-start) | async-done | bytes 688160 | tf_op jit(solution)/shard_map/all_to_all | solution.py:23
  26.4 0.5 broadcast.53
  26.9 2.3 %reduce = f32[32,5376]{1,0:T(8,128)S(1)} reduce(f32[32,1,5376]{2,1,0:T(1,128)S(1)} %all-to-all-done, f32[]{:T(128)} %broadcast.53), dimensions={1}, to_apply=%all_to_all.6.reduce_sub_computation | reduce | bytes 1376260 | tf_op jit(solution)/shard_map/all_to_all | solution.py:23
  29.2 0.8 reshape.50
  30.0 1.7 %bitcast_bitcast_fusion = f32[32,7,32,24]{0,3,1,2:T(8,128)} fusion(f32[32,7,24,32]{3,2,1,0:T(8,128)S(1)} %reshape.50), kind=kLoop, calls=%fused_computation.64 | loop fusion | bytes 1376256 | tf_op jit(solution)/shard_map/transpose | solution.py:16
  31.7 5.6 %copy.21 = f32[32,7,32,24]{3,2,0,1:T(8,128)} copy(f32[32,7,32,24]{0,3,1,2:T(8,128)} %bitcast_bitcast_fusion) | data formatting | bytes 1376256 | tf_op jit(solution)/shard_map/transpose | solution.py:16
  37.3 3.6 %reshape.43 = f32[32,7,768]{2,0,1:T(8,128)S(1)} reshape(f32[32,7,32,24]{3,2,0,1:T(8,128)} %copy.21) | data formatting | bytes 1376256 | tf_op jit(solution)/shard_map/reshape | solution.py:18
  40.9 0.1 constant_dynamic-slice_fusion
  41.0 12.0 %all-gather = f32[128,7,96]{2,0,1:T(8,128)S(1)} all-gather(f32[32,7,96]{2,0,1:T(8,128)S(1)} %constant_dynamic-slice_fusion), channel_id=2, replica_groups=mesh['row'=4,'col_0'=4,'col_1'=4,'col_2'=2] {'row'}, dimensions={0}, use_global_device_ids=true | all-gather | bytes 430080 | tf_op jit(solution)/shard_map/all_gather | solution.py:31
  53.1 0.0 copy-start.1
  53.1 0.0 copy-start.3
  53.1 0.0 copy-start.4
  53.1 0.0 copy-start.5
  53.1 26.3 %multiply_reduce_fusion = (f32[32,768]{1,0:T(8,128)S(1)}, f32[32,768]{1,0:T(8,128)S(1)}) fusion(s32[32,96,768]{2,1,0:T(8,128)} %param.12, f32[32,768]{1,0:T(8,128)S(1)} %get-tuple-element.19, f32[32,96]{1,0:T(8,128)S(1)} %get-tuple-element.26, f32[32,768]{1,0:T(8,128)S(1)} %get-tuple-element.20, f32[32,96]{1,0:T(8,128)S(1)} %get-tuple-element.27, ...), kind=kLoop, calls=%fused_computation.1 | loop fusion | flops 117915648 | bytes 10407936 | tf_op jit(solution)/shard_map/reduce_sum | solution.py:122
  79.5 0.2 copy.22
  79.6 0.9 reshape.51
  80.6 5.6 %all-to-all-start.1 = ((f32[32,1,1536]{2,1,0:T(1,128)}), f32[32,1,1536]{2,1,0:T(1,128)S(1)}, u32[]{:S(2)}, u32[]{:S(2)}) async-start(f32[32,1,1536]{2,1,0:T(1,128)} %reshape.51), calls=%async_computation.1 | async-start | bytes 393216 | tf_op jit(solution)/shard_map/all_to_all | solution.py:41
  86.1 0.0 copy-done.1
  86.1 0.0 copy-done.3
  86.2 0.0 copy-done.4
  86.2 0.3 exponential_reduce_fusion
  86.5 8.0 %all-to-all-done.1 = f32[32,1,1536]{2,1,0:T(1,128)S(1)} async-done(((f32[32,1,1536]{2,1,0:T(1,128)}), f32[32,1,1536]{2,1,0:T(1,128)S(1)}, u32[]{:S(2)}, u32[]{:S(2)}) %all-to-all-start.1) | async-done | bytes 196640 | tf_op jit(solution)/shard_map/all_to_all | solution.py:41
  94.5 1.1 reduce.1
  95.6 0.1 reshape.52
  95.8 0.1 fusion.31
  95.8 0.0 copy-start.2
  95.9 0.1 copy.23
  95.9 0.0 copy-done.5
  95.9 0.6 fusion.35
  96.6 0.6 fusion.34
  97.2 0.7 copy.24
  97.8 9.7 %all-reduce.2 = (f32[]{:T(128)}, f32[]{:T(128)}) all-reduce(f32[]{:T(128)} %get-tuple-element.16, f32[]{:T(128)} %get-tuple-element.32), channel_id=1, replica_groups=mesh['row'=4,'col_0'=4,'col_1'=4,'col_2'=2] {'row'}, use_global_device_ids=true, to_apply=%region_9.10 | all-reduce | flops 2 | bytes 16 | tf_op jit(solution)/shard_map/psum | solution.py:56
  107.6 7.4 %all-reduce.1 = (f32[]{:T(128)}, f32[]{:T(128)}) all-reduce(f32[]{:T(128)} %get-tuple-element.12, f32[]{:T(128)} %get-tuple-element.13), channel_id=1, replica_groups=mesh['row'=4,'col_0'=4,'col_1'=4,'col_2'=2] {'col_0'}, use_global_device_ids=true, to_apply=%region_10.11 | all-reduce | flops 2 | bytes 16 | tf_op jit(solution)/shard_map/psum | solution.py:56
  115.0 7.7 %all-reduce = (f32[]{:T(128)}, f32[]{:T(128)}) all-reduce(f32[]{:T(128)} %get-tuple-element.10, f32[]{:T(128)} %get-tuple-element.11), channel_id=1, replica_groups=mesh['row'=4,'col_0'=4,'col_1'=4,'col_2'=2] {'col_1'}, use_global_device_ids=true, to_apply=%region_11.12 | all-reduce | flops 2 | bytes 16 | tf_op jit(solution)/shard_map/psum | solution.py:56
  122.7 9.1 %all-reduce.3 = (f32[]{:T(128)}, f32[]{:T(128)}) all-reduce(f32[]{:T(128)} %get-tuple-element.8, f32[]{:T(128)} %get-tuple-element.9), channel_id=1, replica_groups=mesh['row'=4,'col_0'=4,'col_1'=4,'col_2'=2] {'col_2'}, use_global_device_ids=true, to_apply=%region_12.13 | all-reduce | flops 2 | bytes 16 | tf_op jit(solution)/shard_map/psum | solution.py:56
  133.0 0.0 copy-done.2
  (8 shorter events, 0.1 us)
Async XLA Ops:
  0.6 15.7 %copy-start = (bf16[384,128]{1,0:T(8,128)(2,1)S(1)}, bf16[384,128]{1,0:T(8,128)(2,1)}, u32[]{:S(2)}) copy-start(bf16[384,128]{1,0:T(8,128)(2,1)} %param.18) | copy-start | bytes 294916
  4.6 21.8 %all-to-all-start = ((f32[32,1,5376]{2,1,0:T(1,128)}), f32[32,1,5376]{2,1,0:T(1,128)S(1)}, u32[]{:S(2)}, u32[]{:S(2)}) async-start(f32[32,1,5376]{2,1,0:T(1,128)} %reshape.49), calls=%async_computation | async-start | bytes 1376256 | tf_op jit(solution)/shard_map/all_to_all | solution.py:23
  53.1 33.1 %copy-start.1 = (bf16[32,24,128]{2,1,0:T(8,128)(2,1)S(1)}, bf16[32,24,128]{2,1,0:T(8,128)(2,1)}, u32[]{:S(2)}) copy-start(bf16[32,24,128]{2,1,0:T(8,128)(2,1)} %fusion.12) | copy-start | bytes 589828
  53.1 33.1 %copy-start.3 = (bf16[128,50]{0,1:T(8,128)(2,1)S(1)}, bf16[128,50]{0,1:T(8,128)(2,1)}, u32[]{:S(2)}) copy-start(bf16[128,50]{0,1:T(8,128)(2,1)} %param.22) | copy-start | bytes 38404
  53.1 33.1 %copy-start.4 = (f32[50]{0:T(128)S(1)}, f32[50]{0:T(128)}, u32[]{:S(2)}) copy-start(f32[50]{0:T(128)} %param.23) | copy-start | bytes 604
  53.1 42.8 %copy-start.5 = (f32[50]{0:T(128)S(1)}, f32[50]{0:T(128)}, u32[]{:S(2)}) copy-start(f32[50]{0:T(128)} %add_multiply_fusion) | copy-start | bytes 604
  80.6 13.9 %all-to-all-start.1 = ((f32[32,1,1536]{2,1,0:T(1,128)}), f32[32,1,1536]{2,1,0:T(1,128)S(1)}, u32[]{:S(2)}, u32[]{:S(2)}) async-start(f32[32,1,1536]{2,1,0:T(1,128)} %reshape.51), calls=%async_computation.1 | async-start | bytes 393216 | tf_op jit(solution)/shard_map/all_to_all | solution.py:41
  95.8 37.2 %copy-start.2 = (f32[32,24]{0,1:T(8,128)}, f32[32,24]{0,1:T(8,128)S(1)}, u32[]{:S(2)}) copy-start(f32[32,24]{0,1:T(8,128)S(1)} %fusion.31) | copy-start | bytes 9220
where the time goes:
time: 135 us; the launch traced here: 134 us
  blocking collectives  45.9 us (34%)
  other arithmetic  35 us (26%)
  local copies, waits for them, and re-layouts  17.4 us (13%)
  waiting for transfers between devices  15.4 us (11%)
  starting transfers between devices  14.2 us (11%)
  between operations  3.24 us (2%)
  matrix products  2.91 us (2%)
    psum x4, blocking collectives, over_axes(): shard = lax.psum(shard, axis)  33.9 us
    reduce_sum x1, other arithmetic, local(): preserved = jnp.sum(weights * scores, axis=1)  26.3 us
    all_gather x1, blocking collectives, from_root(): lax.all_gather(shard, axis)  12 us
    all_to_all x1, starting transfers between devices, sent_to_all(): return lax.all_to_all(copies, axis, split_axis=0, concat_axis=0, tiled=True)  8.58 us
    all_to_all x1, waiting for transfers between devices, summed_on_arrival(): parts = lax.all_to_all(split_up(shard, dim, size), axis, 0, 0, tiled=True)  7.99 us
    all_to_all x1, waiting for transfers between devices, sent_to_all(): return lax.all_to_all(copies, axis, split_axis=0, concat_axis=0, tiled=True)  7.45 us
    transpose x2, local copies, waits for them, and re-layouts, in_order(): parts = jnp.moveaxis(parts, 0, dim)  7.29 us
    unnamed x19, local copies, waits for them, and re-layouts  5.59 us
  transfers between devices with their start and end apart: 2, of which 2 were waited for; matrix products, arithmetic and copies ran while one was open for 5% of the time, Pallas kernels for 0%

commit v1 on v0

v1 whole, which is shorter than its diff:
```python
import functools

import jax
import jax.numpy as jnp
from jax import lax
from jax.experimental import pallas as pl
from jax.experimental.pallas import tpu as pltpu
from jax.sharding import PartitionSpec as P

B = 32
L = 3072
ROWS = 768
COLS = 96
OWN = 24
HALF = 384
BINS = 50
MESH = pl.DeviceIdType.MESH
SPLIT = 12


def plane(x, y, k):
    return x * 8 + y * 2 + k


def kernel(
    n_hbm, tc_hbm, pc_hbm, mask_hbm, single_hbm, gain_hbm, wh_hbm, bh_hbm, wm_hbm, bm_hbm, wl_hbm, bl_hbm,
    lddt_out, loss_out, total_out,
    nbuf, tc, pc, mask, single, gain, wh, bh, wm, bm, wl, bl,
    blk, rows, zbuf, colbuf, rt, logits, stats, logz, pr, rs_send, rs_recv, ar_send, ar_buf,
    in_sem, n_sem, w_sem, z_ssem, z_rsem, c_ssem, c_rsem, g_ssem, g_rsem, f_ssem, f_rsem,
    rs_ssem, rs_rsem, ar_ssem, ar_rsem,
):
    z = lax.axis_index("row")
    c = lax.axis_index("col")
    x = lax.div(c, 8)
    y = lax.rem(lax.div(c, 2), 4)
    k = lax.rem(c, 2)
    half = lax.div(x, 2)
    other = 1 - half
    partner = plane(x, y, 1 - k)
    lane = lax.broadcasted_iota(jnp.int32, (1, 128), 1)

    barrier = pltpu.get_barrier_semaphore()
    starts = [
        pltpu.make_async_copy(tc_hbm, tc, in_sem.at[0]),
        pltpu.make_async_copy(pc_hbm, pc, in_sem.at[1]),
        pltpu.make_async_copy(mask_hbm, mask, in_sem.at[2]),
    ]
    for s in starts:
        s.start()
    for d in range(1, 4):
        pl.semaphore_signal(barrier, inc=1, device_id=(lax.rem(z + d, 4), c), device_id_type=MESH)
    for d in range(1, 32):
        pl.semaphore_signal(barrier, inc=1, device_id=(z, lax.rem(c + d, 32)), device_id_type=MESH)
    head = [
        pltpu.make_async_copy(a, b, w_sem.at[i])
        for i, (a, b) in enumerate(
            [(single_hbm, single), (gain_hbm, gain), (wh_hbm, wh), (bh_hbm, bh), (wm_hbm, wm), (bm_hbm, bm), (wl_hbm, wl), (bl_hbm, bl)]
        )
    ]
    for s in head:
        s.start()
    n_copies = [pltpu.make_async_copy(n_hbm.at[pl.ds(i * 4, 4)], nbuf.at[pl.ds(i * 4, 4)], n_sem.at[i]) for i in range(8)]
    for s in n_copies:
        s.start()
    for s in starts:
        s.wait()
    valid = mask[...].astype(jnp.float32)
    for i in range(3):
        blk[0, :, i * 32 : (i + 1) * 32] = tc[i] * 2.0
        blk[1, :, i * 32 : (i + 1) * 32] = pc[i] * 2.0
    blk[0, :, 96:128] = valid
    blk[1, :, 96:128] = valid
    own_rows = pl.ds(pl.multiple_of(c * OWN, 8), OWN)
    rows[:, own_rows, :] = blk[...]
    pl.semaphore_wait(barrier, 34)

    def z_copy(d):
        return pltpu.make_async_remote_copy(
            blk, zbuf.at[d], z_ssem.at[d], z_rsem.at[d], device_id=(lax.rem(z + 4 - d, 4), c), device_id_type=MESH
        )

    for d in range(1, 4):
        z_copy(d).start()
    slot = lax.rem(y, 2) * 2 + k
    slot_rows = pl.ds(pl.multiple_of(slot * OWN, 8), OWN)

    def col_send(src, d):
        zz = lax.rem(z + d, 4)
        to = plane(zz, x, lax.div(y, 2))
        copy = pltpu.make_async_remote_copy(
            src, colbuf.at[:, slot_rows, :], c_ssem.at[d], c_rsem.at[slot], device_id=(z, to), device_id_type=MESH
        )
        return to, copy

    def col_start(src, d):
        to, copy = col_send(src, d)

        @pl.when(to != c)
        def _():
            copy.start()

        @pl.when(to == c)
        def _():
            colbuf[:, slot_rows, :] = src[...]

    def row_copy(d):
        xx = jnp.where(d < 8, half, other) * 2 + lax.rem(x + lax.rem(lax.div(d, 4), 2), 2)
        to = plane(xx, lax.rem(y + lax.rem(d, 4), 4), k)
        return pltpu.make_async_remote_copy(
            blk, rows.at[:, own_rows, :], g_ssem.at[d], g_rsem.at[c], device_id=(z, to), device_id_type=MESH
        )

    def row_source(d):
        xx = jnp.where(d < 8, half, other) * 2 + lax.rem(x + lax.rem(lax.div(d, 4), 2), 2)
        return plane(xx, lax.rem(y + lax.rem(d, 4), 4), k)

    def forward(src_c, d):
        at = pl.ds(pl.multiple_of(src_c * OWN, 8), OWN)
        sem = 0 if d < 8 else 1
        return pltpu.make_async_remote_copy(
            rows.at[:, at, :], rows.at[:, at, :], f_ssem.at[sem], f_rsem.at[sem], device_id=(z, partner), device_id_type=MESH
        )

    def row_arrival(src_c, d):
        at = pl.ds(pl.multiple_of(src_c * OWN, 8), OWN)
        pltpu.make_async_remote_copy(
            rows.at[:, at, :], rows.at[:, at, :], g_ssem.at[d], g_rsem.at[src_c], device_id=(z, partner), device_id_type=MESH
        ).wait_recv()

    col_start(blk, 0)
    pltpu.make_async_remote_copy(
        blk, rows.at[:, own_rows, :], f_ssem.at[0], f_rsem.at[0], device_id=(z, partner), device_id_type=MESH
    ).start()
    for d in range(1, 16):
        row_copy(d).start()

    for s in head:
        s.wait()
    feats = single[...].astype(jnp.float32)
    average = jnp.sum(feats, axis=-1, keepdims=True) * (1.0 / 384)
    centred = feats - average
    variance = jnp.sum(centred * centred, axis=-1, keepdims=True) * (1.0 / 384)
    normed = (centred * lax.rsqrt(variance + 1e-05) * gain[...]).astype(jnp.bfloat16)
    first = jnp.maximum(jnp.dot(normed, wh[...], preferred_element_type=jnp.float32) + bh[...], 0.0).astype(jnp.bfloat16)
    second = jnp.maximum(jnp.dot(first, wm[...], preferred_element_type=jnp.float32) + bm[...], 0.0).astype(jnp.bfloat16)
    for g in range(6):
        at = lax.broadcasted_iota(jnp.int32, (1, 128), 1) + g * 128
        source = lax.bitwise_and(at, 31) * OWN + lax.shift_right_logical(at, 5)
        pick = (lax.broadcasted_iota(jnp.int32, (ROWS, 128), 0) == source).astype(jnp.float32).astype(jnp.bfloat16)
        moved = lax.dot_general(second, pick, (((0,), (0,)), ((), ())), preferred_element_type=jnp.float32)
        logits[:, g * 128 : (g + 1) * 128] = jnp.dot(wl[...], moved.astype(jnp.bfloat16), preferred_element_type=jnp.float32)
    eye = lax.broadcasted_iota(jnp.int32, (BINS, BINS), 0) == lax.broadcasted_iota(jnp.int32, (BINS, BINS), 1)
    bias = jnp.sum(jnp.where(eye, bl[...], 0.0), axis=1, keepdims=True)
    with_bias = logits[...] + bias
    logits[...] = with_bias
    top = jnp.max(with_bias, axis=0, keepdims=True)
    logz[...] = top + jnp.log(jnp.sum(jnp.exp(with_bias - top), axis=0, keepdims=True))

    for d in range(1, 4):
        z_copy(d).wait_recv()
        col_start(zbuf.at[d], d)
    for d in range(1, 8):
        src_c = row_source(d)
        row_arrival(src_c, d)
        forward(src_c, d).start()

    def forwards_done(sem):
        pltpu.make_async_remote_copy(
            rows.at[:, pl.ds(0, 8 * OWN), :], rows.at[:, pl.ds(0, 8 * OWN), :], f_ssem.at[sem], f_rsem.at[sem],
            device_id=(z, partner), device_id_type=MESH,
        ).wait_recv()

    forwards_done(0)
    for q in range(4):
        src = plane(y, k * 2 + q // 2, q % 2)
        at = pl.ds(q * OWN, OWN)

        @pl.when(src != c)
        def _():
            pltpu.make_async_remote_copy(
                colbuf.at[:, at, :], colbuf.at[:, at, :], c_ssem.at[0], c_rsem.at[q], device_id=(z, partner), device_id_type=MESH
            ).wait_recv()

    for s in n_copies:
        s.wait()

    def turn(h):
        for t in range(2):
            for g in range(3):
                at = pl.ds(pl.multiple_of(h * HALF + g * 128, 128), 128)
                rt[t * 128 : (t + 1) * 128, g * 128 : (g + 1) * 128] = jnp.transpose(rows[t, at, :])

    def pairs(h):
        lanes = pl.ds(pl.multiple_of(h * HALF, 128), HALF)

        def step(b, _):
            r = [rt[pl.ds(t * 128 + i * 32 + b, 1), :] for t in range(2) for i in range(3)]
            shift = lax.rem(128 - b, 128)
            kept = jnp.zeros((8, HALF), jnp.float32)
            count = jnp.zeros((8, HALF), jnp.float32)
            for g in range(12):
                ct = pltpu.roll(colbuf[0, g * 8 : (g + 1) * 8, :], shift, 1)
                cp = pltpu.roll(colbuf[1, g * 8 : (g + 1) * 8, :], shift, 1)
                w = nbuf[b, g * 8 : (g + 1) * 8, lanes].astype(jnp.float32) * ct[:, 96:97]
                dist = []
                for t, cc in ((0, ct), (1, cp)):
                    dx = cc[:, 0:1] - r[t * 3]
                    dy = cc[:, 32:33] - r[t * 3 + 1]
                    dz = cc[:, 64:65] - r[t * 3 + 2]
                    s = dx * dx + dy * dy + dz * dz + 4e-10
                    dist.append(s * lax.rsqrt(s))
                m = jnp.abs(dist[1] - dist[0])
                v = (jnp.tanh(1.0 - m) + jnp.tanh(2.0 - m)) + (jnp.tanh(4.0 - m) + jnp.tanh(8.0 - m))
                kept = kept + w * v
                count = count + w
            kept1 = jnp.sum(kept, axis=0, keepdims=True)
            count1 = jnp.sum(count, axis=0, keepdims=True)
            pr[pl.ds(b, 1), :] = kept1
            pr[pl.ds(b + 32, 1), :] = count1
            pr[pl.ds(b + 64, 1), :] = kept1
            pr[pl.ds(b + 96, 1), :] = count1
            return 0

        return step

    def rs_copy(h, d):
        to = h * 16 + d
        return to, pltpu.make_async_remote_copy(
            rs_send.at[to], rs_recv.at[c], rs_ssem, rs_rsem, device_id=(z, to), device_id_type=MESH
        )

    def share(h):
        low = lane < 64
        tr = [jnp.transpose(pr[:, g * 128 : (g + 1) * 128]) for g in range(3)]
        unit = lambda u: tr[u // 16][(u % 16) * 8 : (u % 16) * 8 + 8, :]
        for d in range(16):
            rs_send[h * 16 + d, 0:8, :] = jnp.where(low, unit(3 * d), unit(3 * d + 1))
            rs_send[h * 16 + d, 8:16, :] = unit(3 * d + 2)

        def go(d, _):
            to, copy = rs_copy(h, d)

            @pl.when(to != c)
            def _():
                copy.start()

            @pl.when(to == c)
            def _():
                rs_recv[c] = rs_send[c]

            return 0

        lax.fori_loop(0, 16, go, 0)

    turn(half)
    lax.fori_loop(0, SPLIT, pairs(half), 0)
    for d in range(8, 16):
        src_c = row_source(d)
        row_arrival(src_c, d)
        forward(src_c, d).start()
    lax.fori_loop(SPLIT, B, pairs(half), 0)
    share(half)
    forwards_done(1)
    turn(other)
    lax.fori_loop(0, B, pairs(other), 0)
    share(other)

    everyone = lambda a, b: pltpu.make_async_remote_copy(
        rs_send.at[pl.ds(0, 31)], rs_recv.at[pl.ds(0, 31)], rs_ssem, rs_rsem, device_id=(z, partner), device_id_type=MESH
    )
    everyone(0, 0).wait_recv()
    packed = jnp.sum(rs_recv[...], axis=0)
    a0, a1 = packed[0:8], packed[8:16]
    kept = jnp.concatenate([a0, pltpu.roll(a0, 64, 1), a1], axis=0)
    count = pltpu.roll(kept, 96, 1)[:, :32] * valid
    kept = kept[:, :32] * valid
    score = (0.5 * count + 0.125 * kept) / jnp.maximum(count, 1.0)
    lddt_out[...] = score
    stats[0:24, 0:32] = score
    stats[0:24, 32:64] = score
    stats[0:24, 64:96] = score
    stats[0:24, 96:128] = score
    stats[24:48, 0:32] = valid
    stats[24:48, 32:64] = valid
    stats[24:48, 64:96] = valid
    stats[24:48, 96:128] = valid
    group = lax.shift_right_logical(lane, 5)
    centers = (lax.broadcasted_iota(jnp.int32, (BINS, 1), 0).astype(jnp.float32) + 0.5) * (1.0 / BINS)
    loss_sum = jnp.zeros((1, 128), jnp.float32)
    valid_sum = jnp.zeros((1, 128), jnp.float32)
    losses = []
    for g in range(6):
        flat = lambda base: jnp.where(
            group == 0,
            stats[base + 4 * g : base + 4 * g + 1, :],
            jnp.where(
                group == 1,
                stats[base + 4 * g + 1 : base + 4 * g + 2, :],
                jnp.where(group == 2, stats[base + 4 * g + 2 : base + 4 * g + 3, :], stats[base + 4 * g + 3 : base + 4 * g + 4, :]),
            ),
        )
        value, keep = flat(0), flat(24)
        off = value - centers
        near = jnp.exp(off * off * (-(BINS * BINS * 0.5)))
        block = logits[:, g * 128 : (g + 1) * 128]
        mean = jnp.sum(near * block, axis=0, keepdims=True) / jnp.sum(near, axis=0, keepdims=True)
        loss = keep * (logz[:, g * 128 : (g + 1) * 128] - mean)
        losses.append(loss)
        loss_sum = loss_sum + loss
        valid_sum = valid_sum + keep
    both = jnp.where(lane < 64, loss_sum + pltpu.roll(loss_sum, 64, 1), valid_sum + pltpu.roll(valid_sum, 64, 1))
    ar_send[...] = both
    me = z * 32 + c
    ar_buf[pl.ds(me, 1)] = both.reshape(1, 1, 128)
    for d in (2, 1, 3, 0):
        zz = lax.rem(z + d, 4)

        def tell(i, _):
            pltpu.make_async_remote_copy(
                ar_send, ar_buf.at[me], ar_ssem, ar_rsem, device_id=(zz, lax.rem(c + i, 32)), device_id_type=MESH
            ).start()
            return 0

        lax.fori_loop(0 if d else 1, 32, tell, 0)
    for g in range(6):
        for t in range(4):
            part = pltpu.roll(losses[g], (128 - 32 * t) % 128, 1) if t else losses[g]
            loss_out[4 * g + t : 4 * g + t + 1, :] = part[:, :32]

    for d in range(1, 4):
        z_copy(d).wait_send()
    for d in range(4):
        to, copy = col_send(blk, d)

        @pl.when(to != c)
        def _():
            copy.wait_send()

    for d in range(1, 16):
        row_copy(d).wait_send()
    for sem in range(2):
        pltpu.make_async_remote_copy(
            rows.at[:, pl.ds(0, 8 * OWN), :], rows.at[:, pl.ds(0, 8 * OWN), :], f_ssem.at[sem], f_rsem.at[sem],
            device_id=(z, partner), device_id_type=MESH,
        ).wait_send()
    everyone(0, 0).wait_send()
    last = pltpu.make_async_remote_copy(
        ar_buf.at[pl.ds(0, 127)], ar_buf.at[pl.ds(0, 127)], ar_ssem, ar_rsem, device_id=(z, partner), device_id_type=MESH
    )
    last.wait_recv()
    everything = jnp.sum(ar_buf[...], axis=0)
    loss_total = jnp.sum(jnp.where(lane < 64, everything, 0.0), axis=1, keepdims=True)
    valid_total = jnp.sum(jnp.where(lane < 64, 0.0, everything), axis=1, keepdims=True)
    total_out[...] = loss_total / valid_total
    last.wait_send()


def local(neighbor, true_coords, pred_coords, residue_mask, single, ln_gain, w_hidden, b_hidden, w_mid, b_mid, w_logits, b_logits):
    f32, bf16 = jnp.float32, jnp.bfloat16
    anywhere = pl.BlockSpec(memory_space=pl.ANY)
    in_vmem = pl.BlockSpec(memory_space=pltpu.VMEM)
    dma = pltpu.SemaphoreType.DMA
    score, loss, total = pl.pallas_call(
        kernel,
        out_shape=(
            jax.ShapeDtypeStruct((OWN, B), f32),
            jax.ShapeDtypeStruct((OWN, B), f32),
            jax.ShapeDtypeStruct((1, 1), f32),
        ),
        in_specs=[anywhere] * 12,
        out_specs=(in_vmem, in_vmem, in_vmem),
        scratch_shapes=[
            pltpu.VMEM((B, COLS, ROWS), jnp.int32),
            pltpu.VMEM((3, OWN, B), f32),
            pltpu.VMEM((3, OWN, B), f32),
            pltpu.VMEM((OWN, B), jnp.int32),
            pltpu.VMEM((ROWS, 384), bf16),
            pltpu.VMEM((1, 384), f32),
            pltpu.VMEM((384, 128), bf16),
            pltpu.VMEM((1, 128), f32),
            pltpu.VMEM((128, 128), bf16),
            pltpu.VMEM((1, 128), f32),
            pltpu.VMEM((BINS, 128), bf16),
            pltpu.VMEM((1, BINS), f32),
            pltpu.VMEM((2, OWN, 128), f32),
            pltpu.VMEM((2, ROWS, 128), f32),
            pltpu.VMEM((4, 2, OWN, 128), f32),
            pltpu.VMEM((2, COLS, 128), f32),
            pltpu.VMEM((256, HALF), f32),
            pltpu.VMEM((BINS, ROWS), f32),
            pltpu.VMEM((48, 128), f32),
            pltpu.VMEM((1, ROWS), f32),
            pltpu.VMEM((128, HALF), f32),
            pltpu.VMEM((32, 16, 128), f32),
            pltpu.VMEM((32, 16, 128), f32),
            pltpu.VMEM((1, 128), f32),
            pltpu.VMEM((128, 1, 128), f32),
            dma((3,)), dma((8,)), dma((8,)), dma((4,)), dma((4,)), dma((4,)), dma((4,)), dma((16,)), dma((32,)), dma((2,)), dma((2,)),
            dma, dma, dma, dma,
        ],
        compiler_params=pltpu.CompilerParams(collective_id=0, has_side_effects=True, vmem_limit_bytes=48 * 1024 * 1024),
    )(
        neighbor,
        jnp.transpose(true_coords, (1, 2, 0)),
        jnp.transpose(pred_coords, (1, 2, 0)),
        residue_mask.T,
        single.reshape(ROWS, 384),
        ln_gain.reshape(1, 384),
        w_hidden,
        b_hidden.reshape(1, 128),
        w_mid,
        b_mid.reshape(1, 128),
        w_logits.T,
        b_logits.reshape(1, BINS),
    )
    return score.T, loss.T, total.reshape(())


def solution(mesh):
    placed = (
        P(None, "col", "row"),
        P(None, None, ("row", "col")),
        P(None, None, ("row", "col")),
        P(None, ("row", "col")),
        P(None, ("row", "col"), None),
    ) + (P(),) * 7
    return jax.shard_map(
        local,
        mesh=mesh,
        in_specs=placed,
        out_specs=(P(None, ("row", "col")), P(None, ("row", "col")), P()),
        check_vma=False,
    )
```

time: 135 us -> 70.6 us (0.52)
  Pallas kernels: 0 us -> 58.1 us
  blocking collectives: 45.9 us -> 0 us
  other arithmetic: 35 us -> 0 us
  waiting for transfers between devices: 15.4 us -> 0 us
  starting transfers between devices: 14.2 us -> 0 us
  local copies, waits for them, and re-layouts: 17.4 us -> 9.52 us
  matrix products: 2.91 us -> 0 us
    pallas_call x0 -> x1, Pallas kernels: none -> 58.1 us  [local(): pl.pallas_call(kernel, out_shape=(jax.ShapeDtypeStruct((OWN, B), f32), ja...]
    psum x4 -> x0, blocking collectives: 33.9 us -> none  [over_axes(): shard = lax.psum(shard, axis)]
    reduce_sum x5 -> x0, other arithmetic: 29.6 us -> none  [the longest x1 26.3 us: local(): preserved = jnp.sum(weights * scores, axis=1)]
    all_to_all x2 -> x0, waiting for transfers between devices: 15.4 us -> none  [the longest x1 7.99 us: summed_on_arrival(): parts = lax.all_to_all(split_up(shard, dim, size), axis, 0, 0, tiled=True)]
    all_to_all x2 -> x0, starting transfers between devices: 14.2 us -> none  [the longest x1 8.58 us: sent_to_all(): return lax.all_to_all(copies, axis, split_axis=0, concat_axis=0, tiled=True)]
    all_gather x1 -> x0, blocking collectives: 12 us -> none  [from_root(): lax.all_gather(shard, axis)]
    transpose x2 -> x0, local copies, waits for them, and re-layouts: 7.29 us -> none  [in_order(): parts = jnp.moveaxis(parts, 0, dim)]
    all_to_all x2 -> x0, other arithmetic: 3.37 us -> none  [the longest x1 2.27 us: sent_to_all(): return lax.all_to_all(copies, axis, split_axis=0, concat_axis=0, tiled=True)]
  transfers between devices with their start and end apart: 2 -> 0, of which waited for: 2 -> 0; matrix products, arithmetic and copies ran while one was open for 5% -> 0% of each run, Pallas kernels for 0% -> 0%
where the time goes in v1:
time: 70.6 us; the launch traced here: 70 us
  Pallas kernels  58.1 us (82%)
  local copies, waits for them, and re-layouts  9.52 us (13%)
  between operations  2.41 us (3%)
    pallas_call x1, Pallas kernels, local(): pl.pallas_call(kernel, out_shape=(jax.ShapeDtypeStruct((OWN, B), f32), ja...  58.1 us
    unnamed x22, local copies, waits for them, and re-layouts  8.83 us

profile of v1, /device:TPU:1, one launch (start us, length us, event | category | flops | bytes accessed | tf_op | source)
XLA Modules:
  0.0 70.0 jit_solution(10912807591263953121)
XLA Ops:
  0.6 0.7 reshape.25.gain_hbm
  1.3 0.0 copy-start
  1.3 1.1 %copy-done = bf16[32,24,384]{2,1,0:T(8,128)(2,1)S(1)} copy-done((bf16[32,24,384]{2,1,0:T(8,128)(2,1)S(1)}, bf16[32,24,384]{2,1,0:T(8,128)(2,1)}, u32[]{:S(2)}) %copy-start) | copy-done | bytes 589848
  2.4 0.0 copy-start.1
  2.4 0.9 %copy-done.1 = bf16[384,128]{1,0:T(8,128)(2,1)S(1)} copy-done((bf16[384,128]{1,0:T(8,128)(2,1)S(1)}, bf16[384,128]{1,0:T(8,128)(2,1)}, u32[]{:S(2)}) %copy-start.1) | copy-done | bytes 98328
  3.3 0.0 copy-start.2
  3.3 0.8 %copy-done.2 = f32[32,3,24]{0,2,1:T(8,128)S(1)} copy-done((f32[32,3,24]{0,2,1:T(8,128)S(1)}, f32[32,3,24]{0,2,1:T(8,128)}, u32[]{:S(2)}) %copy-start.2) | copy-done | bytes 9240
  4.0 0.0 copy-start.3
  4.0 0.8 %copy-done.3 = f32[32,3,24]{0,2,1:T(8,128)S(1)} copy-done((f32[32,3,24]{0,2,1:T(8,128)S(1)}, f32[32,3,24]{0,2,1:T(8,128)}, u32[]{:S(2)}) %copy-start.3) | copy-done | bytes 9240
  4.8 0.0 copy-start.4
  4.8 0.8 %copy-done.4 = bf16[128,128]{1,0:T(8,128)(2,1)S(1)} copy-done((bf16[128,128]{1,0:T(8,128)(2,1)S(1)}, bf16[128,128]{1,0:T(8,128)(2,1)}, u32[]{:S(2)}) %copy-start.4) | copy-done | bytes 32792
  5.6 0.0 copy-start.5
  5.6 0.7 %copy-done.5 = bf16[128,50]{0,1:T(8,128)(2,1)S(1)} copy-done((bf16[128,50]{0,1:T(8,128)(2,1)S(1)}, bf16[128,50]{0,1:T(8,128)(2,1)}, u32[]{:S(2)}) %copy-start.5) | copy-done | bytes 12824
  6.3 0.0 copy-start.6
  6.3 0.7 %copy-done.6 = s32[32,24]{0,1:T(8,128)S(1)} copy-done((s32[32,24]{0,1:T(8,128)S(1)}, s32[32,24]{0,1:T(8,128)}, u32[]{:S(2)}) %copy-start.6) | copy-done | bytes 3096
  7.0 0.0 copy-start.7
  7.0 0.7 copy-done.7
  7.6 0.0 copy-start.8
  7.6 0.7 copy-done.8
  8.3 0.0 copy-start.9
  8.3 0.7 copy-done.9
  9.0 58.1 %shard_map.139 = (f32[24,32]{1,0:T(8,128)S(1)}, f32[24,32]{1,0:T(8,128)S(1)}, f32[1,1]{1,0:T(1,128)}) custom-call(s32[32,96,768]{2,1,0:T(8,128)} %n_hbm.1, f32[3,24,32]{2,1,0:T(8,128)S(1)} %bitcast.12, f32[3,24,32]{2,1,0:T(8,128)S(1)} %bitcast.13, s32[24,32]{1,0:T(8,128)S(1)} %bitcast.15, bf16[768,384]{1,0:T(8,128)(2,1)S(1)} %bitcast.11, ...), custom_call_target="tpu_custom_call" | custom-call | tf_op jit(solution)/shard_map/pallas_call | solution.py:364
  67.1 0.6 copy.18
  67.7 0.6 copy.19
Async XLA Ops:
  1.3 1.1 %copy-start = (bf16[32,24,384]{2,1,0:T(8,128)(2,1)S(1)}, bf16[32,24,384]{2,1,0:T(8,128)(2,1)}, u32[]{:S(2)}) copy-start(bf16[32,24,384]{2,1,0:T(8,128)(2,1)} %param.16) | copy-start | bytes 1769476
  2.4 0.9 %copy-start.1 = (bf16[384,128]{1,0:T(8,128)(2,1)S(1)}, bf16[384,128]{1,0:T(8,128)(2,1)}, u32[]{:S(2)}) copy-start(bf16[384,128]{1,0:T(8,128)(2,1)} %wh_hbm.1) | copy-start | bytes 294916
  3.3 0.8 %copy-start.2 = (f32[32,3,24]{0,2,1:T(8,128)S(1)}, f32[32,3,24]{0,2,1:T(8,128)}, u32[]{:S(2)}) copy-start(f32[32,3,24]{0,2,1:T(8,128)} %param.13) | copy-start | bytes 27652
  4.0 0.8 %copy-start.3 = (f32[32,3,24]{0,2,1:T(8,128)S(1)}, f32[32,3,24]{0,2,1:T(8,128)}, u32[]{:S(2)}) copy-start(f32[32,3,24]{0,2,1:T(8,128)} %param.14) | copy-start | bytes 27652
  4.8 0.8 %copy-start.4 = (bf16[128,128]{1,0:T(8,128)(2,1)S(1)}, bf16[128,128]{1,0:T(8,128)(2,1)}, u32[]{:S(2)}) copy-start(bf16[128,128]{1,0:T(8,128)(2,1)} %wm_hbm.1) | copy-start | bytes 98308
  5.6 0.7 %copy-start.5 = (bf16[128,50]{0,1:T(8,128)(2,1)S(1)}, bf16[128,50]{0,1:T(8,128)(2,1)}, u32[]{:S(2)}) copy-start(bf16[128,50]{0,1:T(8,128)(2,1)} %param.22) | copy-start | bytes 38404
  6.3 0.7 %copy-start.6 = (s32[32,24]{0,1:T(8,128)S(1)}, s32[32,24]{0,1:T(8,128)}, u32[]{:S(2)}) copy-start(s32[32,24]{0,1:T(8,128)} %param.15) | copy-start | bytes 9220
  7.0 0.7 copy-start.7
  7.6 0.7 copy-start.8
  8.3 0.7 copy-start.9

commit v2 on v1

--- a/solution.py
+++ b/solution.py
@@ -15,7 +15,8 @@
 HALF = 384
 BINS = 50
 MESH = pl.DeviceIdType.MESH
-SPLIT = 12
+SPLIT = 3
+PITCH = 33
 
 
 def plane(x, y, k):
@@ -24,11 +25,11 @@
 
 def kernel(
     n_hbm, tc_hbm, pc_hbm, mask_hbm, single_hbm, gain_hbm, wh_hbm, bh_hbm, wm_hbm, bm_hbm, wl_hbm, bl_hbm,
-    lddt_out, loss_out, total_out,
+    out,
     nbuf, tc, pc, mask, single, gain, wh, bh, wm, bm, wl, bl,
-    blk, rows, zbuf, colbuf, rt, logits, stats, logz, pr, rs_send, rs_recv, ar_send, ar_buf,
+    blk, rows, zbuf, colbuf, pick_left, left, right, dist, logits, stats, logz, pr, rs_send, rs_recv, ar_send, ar_buf,
     in_sem, n_sem, w_sem, z_ssem, z_rsem, c_ssem, c_rsem, g_ssem, g_rsem, f_ssem, f_rsem,
-    rs_ssem, rs_rsem, ar_ssem, ar_rsem,
+    rs_ssem, rs_rsem, ar_ssem, ar_rsem, far_in,
 ):
     z = lax.axis_index("row")
     c = lax.axis_index("col")
@@ -48,10 +49,13 @@
     ]
     for s in starts:
         s.start()
+    near = lax.div(x, 2) * 16
     for d in range(1, 4):
         pl.semaphore_signal(barrier, inc=1, device_id=(lax.rem(z + d, 4), c), device_id_type=MESH)
-    for d in range(1, 32):
-        pl.semaphore_signal(barrier, inc=1, device_id=(z, lax.rem(c + d, 32)), device_id_type=MESH)
+    for d in range(1, 16):
+        pl.semaphore_signal(barrier, inc=1, device_id=(z, near + lax.rem(c + d, 16)), device_id_type=MESH)
+    mirror = lax.rem(c + 16, 32)
+    pl.semaphore_signal(barrier, inc=1, device_id=(z, mirror), device_id_type=MESH)
     head = [
         pltpu.make_async_copy(a, b, w_sem.at[i])
         for i, (a, b) in enumerate(
@@ -73,7 +77,8 @@
     blk[1, :, 96:128] = valid
     own_rows = pl.ds(pl.multiple_of(c * OWN, 8), OWN)
     rows[:, own_rows, :] = blk[...]
-    pl.semaphore_wait(barrier, 34)
+    pl.semaphore_wait(barrier, 19)
+    pl.semaphore_signal(far_in, inc=1, device_id=(z, mirror), device_id_type=MESH)
 
     def z_copy(d):
         return pltpu.make_async_remote_copy(
@@ -128,20 +133,23 @@
             rows.at[:, at, :], rows.at[:, at, :], g_ssem.at[d], g_rsem.at[src_c], device_id=(z, partner), device_id_type=MESH
         ).wait_recv()
 
-    col_start(blk, 0)
     pltpu.make_async_remote_copy(
         blk, rows.at[:, own_rows, :], f_ssem.at[0], f_rsem.at[0], device_id=(z, partner), device_id_type=MESH
     ).start()
-    for d in range(1, 16):
+    for d in range(1, 8):
         row_copy(d).start()
 
+    pl.semaphore_wait(far_in, 1)
+    col_start(blk, 0)
+    for d in range(8, 16):
+        row_copy(d).start()
     for s in head:
         s.wait()
     feats = single[...].astype(jnp.float32)
     average = jnp.sum(feats, axis=-1, keepdims=True) * (1.0 / 384)
     centred = feats - average
     variance = jnp.sum(centred * centred, axis=-1, keepdims=True) * (1.0 / 384)
-    normed = (centred * lax.rsqrt(variance + 1e-05) * gain[...]).astype(jnp.bfloat16)
+    normed = (centred * lax.rsqrt(variance + 1e-05) * gain[...].reshape(1, 384)).astype(jnp.bfloat16)
     first = jnp.maximum(jnp.dot(normed, wh[...], preferred_element_type=jnp.float32) + bh[...], 0.0).astype(jnp.bfloat16)
     second = jnp.maximum(jnp.dot(first, wm[...], preferred_element_type=jnp.float32) + bm[...], 0.0).astype(jnp.bfloat16)
     for g in range(6):
@@ -157,6 +165,20 @@
     top = jnp.max(with_bias, axis=0, keepdims=True)
     logz[...] = top + jnp.log(jnp.sum(jnp.exp(with_bias - top), axis=0, keepdims=True))
 
+    for i in range(16):
+        at = lax.broadcasted_iota(jnp.int32, (1, 128), 1) + i * 128
+        b_of = lax.shift_right_logical(at, 6)
+        q = lax.bitwise_and(lax.shift_right_logical(at, 4), 3)
+        p = lax.bitwise_and(lax.shift_right_logical(at, 2), 3)
+        part = lax.bitwise_and(at, 3)
+        source = jnp.where(
+            (p < 3) & (q < 3) & ((part < 3) | (q == 0)),
+            p * 128 + part * 32 + b_of,
+            jnp.where((part == 3) & (((q == 1) & (p < 2)) | ((q == 2) & (p == 0))), 384, -1),
+        )
+        hot = (lax.broadcasted_iota(jnp.int32, (512, 128), 0) == source).astype(jnp.float32)
+        pick_left[:, i * 128 : (i + 1) * 128] = hot.astype(jnp.bfloat16)
+
     for d in range(1, 4):
         z_copy(d).wait_recv()
         col_start(zbuf.at[d], d)
@@ -185,41 +207,98 @@
     for s in n_copies:
         s.wait()
 
+    def pieces(v):
+        p0 = v.astype(jnp.bfloat16).astype(jnp.float32)
+        p1 = (v - p0).astype(jnp.bfloat16).astype(jnp.float32)
+        return p0, p1, v - p0 - p1
+
+    def centre(t):
+        return jnp.where(lane < 96, colbuf[t, 0:1, :], 0.0)
+
+    def left_sides():
+        both = []
+        for t in range(2):
+            a = colbuf[t] - centre(t)
+            sq = a * a
+            norm = (pltpu.roll(sq, 96, 1) + pltpu.roll(sq, 64, 1)) + pltpu.roll(sq, 32, 1)
+            parts = pieces(jnp.where(lane < 96, a, norm))
+            both.append(jnp.concatenate([p.astype(jnp.bfloat16) for p in parts] + [jnp.ones((COLS, 128), jnp.bfloat16)], axis=1))
+        both = jnp.concatenate(both, axis=0)
+        for i in range(8):
+            at = slice(i * 256, (i + 1) * 256)
+            left[:, at] = jnp.dot(both, pick_left[:, at], preferred_element_type=jnp.float32).astype(jnp.bfloat16)
+
     def turn(h):
+        one = jnp.full((32, 128), 1.0, jnp.float32)
         for t in range(2):
-            for g in range(3):
-                at = pl.ds(pl.multiple_of(h * HALF + g * 128, 128), 128)
-                rt[t * 128 : (t + 1) * 128, g * 128 : (g + 1) * 128] = jnp.transpose(rows[t, at, :])
+            mid = centre(t)
+            for v in range(3):
+                at = pl.ds(pl.multiple_of(h * HALF + v * 128, 128), 128)
+                flat = jnp.transpose(rows[t, at, :] - mid)
+                xyz = flat[0:96]
+                sq = xyz * xyz
+                m = pieces((sq[0:32] + sq[32:64]) + (sq[64:96] + 4e-10))
+                p = pieces(xyz * -2.0)
+                for q, (u, w) in enumerate(((one, one), (m[0], m[1]), (m[2], m[2]))):
+                    for slot, rows32 in enumerate((p[q][0:32], p[q][32:64], p[q][64:96], u) + (p[q][0:32], p[q][32:64], p[q][64:96], w)):
+                        right[t, q, v, slot * PITCH : slot * PITCH + 32, :] = rows32
+
+    def distances(b, i, s, dst):
+        at = pl.ds(pl.multiple_of(i * 128, 128), 128)
+        for t in range(2):
+            lhs = left[t * COLS : (t + 1) * COLS, at]
+            cols = []
+            for v in range(3):
+                vs = [right[t, q, v, pl.ds(b, 8, stride=PITCH), :] for q in range(3)]
+                cols.append(jnp.concatenate([vs[0], vs[0], vs[1], vs[1], vs[2], vs[2]], axis=0).astype(jnp.bfloat16))
+            rhs = jnp.concatenate(cols, axis=1)
+            if s == 0:
+                rhs = jnp.concatenate([rhs, jnp.zeros((80, HALF), jnp.bfloat16)], axis=0)
+            else:
+                rhs = jnp.concatenate([jnp.zeros((64, HALF), jnp.bfloat16), rhs, jnp.zeros((16, HALF), jnp.bfloat16)], axis=0)
+            dst[t] = jnp.dot(lhs, rhs, preferred_element_type=jnp.float32)
 
     def pairs(h):
-        lanes = pl.ds(pl.multiple_of(h * HALF, 128), HALF)
-
-        def step(b, _):
-            r = [rt[pl.ds(t * 128 + i * 32 + b, 1), :] for t in range(2) for i in range(3)]
+        def one(b, src):
+            kept = [jnp.zeros((8, 128), jnp.float32)] * 3
+            count = [jnp.zeros((8, 128), jnp.float32)] * 3
             shift = lax.rem(128 - b, 128)
-            kept = jnp.zeros((8, HALF), jnp.float32)
-            count = jnp.zeros((8, HALF), jnp.float32)
             for g in range(12):
-                ct = pltpu.roll(colbuf[0, g * 8 : (g + 1) * 8, :], shift, 1)
-                cp = pltpu.roll(colbuf[1, g * 8 : (g + 1) * 8, :], shift, 1)
-                w = nbuf[b, g * 8 : (g + 1) * 8, lanes].astype(jnp.float32) * ct[:, 96:97]
-                dist = []
-                for t, cc in ((0, ct), (1, cp)):
-                    dx = cc[:, 0:1] - r[t * 3]
-                    dy = cc[:, 32:33] - r[t * 3 + 1]
-                    dz = cc[:, 64:65] - r[t * 3 + 2]
-                    s = dx * dx + dy * dy + dz * dz + 4e-10
-                    dist.append(s * lax.rsqrt(s))
-                m = jnp.abs(dist[1] - dist[0])
-                v = (jnp.tanh(1.0 - m) + jnp.tanh(2.0 - m)) + (jnp.tanh(4.0 - m) + jnp.tanh(8.0 - m))
-                kept = kept + w * v
-                count = count + w
-            kept1 = jnp.sum(kept, axis=0, keepdims=True)
-            count1 = jnp.sum(count, axis=0, keepdims=True)
-            pr[pl.ds(b, 1), :] = kept1
-            pr[pl.ds(b + 32, 1), :] = count1
-            pr[pl.ds(b + 64, 1), :] = kept1
-            pr[pl.ds(b + 96, 1), :] = count1
+                cm = jnp.broadcast_to(pltpu.roll(colbuf[0, g * 8 : (g + 1) * 8, :], shift, 1)[:, 96:97], (8, 128))
+                for v in range(3):
+                    lanes = pl.ds(pl.multiple_of(h * HALF + v * 128, 128), 128)
+                    w = nbuf[b, g * 8 : (g + 1) * 8, lanes].astype(jnp.float32) * cm
+                    s0 = jnp.maximum(src[0, g * 8 : (g + 1) * 8, v * 128 : (v + 1) * 128], 4e-10)
+                    s1 = jnp.maximum(src[1, g * 8 : (g + 1) * 8, v * 128 : (v + 1) * 128], 4e-10)
+                    m = jnp.abs(s1 * lax.rsqrt(s1) - s0 * lax.rsqrt(s0))
+                    score = (jnp.tanh(1.0 - m) + jnp.tanh(2.0 - m)) + (jnp.tanh(4.0 - m) + jnp.tanh(8.0 - m))
+                    kept[v] = kept[v] + w * score
+                    count[v] = count[v] + w
+            for v in range(3):
+                kept1 = jnp.sum(kept[v], axis=0, keepdims=True)
+                count1 = jnp.sum(count[v], axis=0, keepdims=True)
+                pr[v, pl.ds(b, 1), :] = kept1
+                pr[v, pl.ds(b + 32, 1), :] = count1
+                pr[v, pl.ds(b + 64, 1), :] = kept1
+                pr[v, pl.ds(b + 96, 1), :] = count1
+
+        def step(i, _):
+            after = jnp.minimum(i + 1, B // 4 - 1)
+
+            def quad(now, later):
+                for j in range(4):
+                    one(4 * i + j, dist.at[now + j])
+                for j in range(4):
+                    distances(4 * after + j, 2 * after + j // 2, j % 2, dist.at[later + j])
+
+            @pl.when(lax.rem(i, 2) == 0)
+            def _():
+                quad(0, 4)
+
+            @pl.when(lax.rem(i, 2) == 1)
+            def _():
+                quad(4, 0)
+
             return 0
 
         return step
@@ -232,13 +311,13 @@
 
     def share(h):
         low = lane < 64
-        tr = [jnp.transpose(pr[:, g * 128 : (g + 1) * 128]) for g in range(3)]
+        tr = [jnp.transpose(pr[g]) for g in range(3)]
         unit = lambda u: tr[u // 16][(u % 16) * 8 : (u % 16) * 8 + 8, :]
         for d in range(16):
             rs_send[h * 16 + d, 0:8, :] = jnp.where(low, unit(3 * d), unit(3 * d + 1))
             rs_send[h * 16 + d, 8:16, :] = unit(3 * d + 2)
 
-        def go(d, _):
+        for d in range(16):
             to, copy = rs_copy(h, d)
 
             @pl.when(to != c)
@@ -249,21 +328,23 @@
             def _():
                 rs_recv[c] = rs_send[c]
 
-            return 0
-
-        lax.fori_loop(0, 16, go, 0)
-
+
+    left_sides()
     turn(half)
+    for j in range(4):
+        distances(j, j // 2, j % 2, dist.at[j])
     lax.fori_loop(0, SPLIT, pairs(half), 0)
     for d in range(8, 16):
         src_c = row_source(d)
         row_arrival(src_c, d)
         forward(src_c, d).start()
-    lax.fori_loop(SPLIT, B, pairs(half), 0)
+    lax.fori_loop(SPLIT, B // 4, pairs(half), 0)
     share(half)
     forwards_done(1)
     turn(other)
-    lax.fori_loop(0, B, pairs(other), 0)
+    for j in range(4):
+        distances(j, j // 2, j % 2, dist.at[j])
+    lax.fori_loop(0, B // 4, pairs(other), 0)
     share(other)
 
     everyone = lambda a, b: pltpu.make_async_remote_copy(
@@ -276,7 +357,7 @@
     count = pltpu.roll(kept, 96, 1)[:, :32] * valid
     kept = kept[:, :32] * valid
     score = (0.5 * count + 0.125 * kept) / jnp.maximum(count, 1.0)
-    lddt_out[...] = score
+    out[0] = score
     stats[0:24, 0:32] = score
     stats[0:24, 32:64] = score
     stats[0:24, 64:96] = score
@@ -313,20 +394,18 @@
     ar_send[...] = both
     me = z * 32 + c
     ar_buf[pl.ds(me, 1)] = both.reshape(1, 1, 128)
-    for d in (2, 1, 3, 0):
-        zz = lax.rem(z + d, 4)
-
-        def tell(i, _):
+    for i in range(128):
+
+        @pl.when(me != i)
+        def _():
             pltpu.make_async_remote_copy(
-                ar_send, ar_buf.at[me], ar_ssem, ar_rsem, device_id=(zz, lax.rem(c + i, 32)), device_id_type=MESH
+                ar_send, ar_buf.at[me], ar_ssem, ar_rsem, device_id=(i // 32, i % 32), device_id_type=MESH
             ).start()
-            return 0
-
-        lax.fori_loop(0 if d else 1, 32, tell, 0)
+
     for g in range(6):
         for t in range(4):
             part = pltpu.roll(losses[g], (128 - 32 * t) % 128, 1) if t else losses[g]
-            loss_out[4 * g + t : 4 * g + t + 1, :] = part[:, :32]
+            out[1, 4 * g + t : 4 * g + t + 1, :] = part[:, :32]
 
     for d in range(1, 4):
         z_copy(d).wait_send()
@@ -352,8 +431,14 @@
     everything = jnp.sum(ar_buf[...], axis=0)
     loss_total = jnp.sum(jnp.where(lane < 64, everything, 0.0), axis=1, keepdims=True)
     valid_total = jnp.sum(jnp.where(lane < 64, 0.0, everything), axis=1, keepdims=True)
-    total_out[...] = loss_total / valid_total
+    out[2] = jnp.broadcast_to(loss_total / valid_total, (OWN, B))
     last.wait_send()
+
+
+def finish(out, score, loss, total):
+    score[...] = out[0]
+    loss[...] = out[1]
+    total[...] = out[2, 0:1, 0:1]
 
 
 def local(neighbor, true_coords, pred_coords, residue_mask, single, ln_gain, w_hidden, b_hidden, w_mid, b_mid, w_logits, b_logits):
@@ -361,22 +446,18 @@
     anywhere = pl.BlockSpec(memory_space=pl.ANY)
     in_vmem = pl.BlockSpec(memory_space=pltpu.VMEM)
     dma = pltpu.SemaphoreType.DMA
-    score, loss, total = pl.pallas_call(
+    out = pl.pallas_call(
         kernel,
-        out_shape=(
-            jax.ShapeDtypeStruct((OWN, B), f32),
-            jax.ShapeDtypeStruct((OWN, B), f32),
-            jax.ShapeDtypeStruct((1, 1), f32),
-        ),
+        out_shape=jax.ShapeDtypeStruct((3, OWN, B), f32),
         in_specs=[anywhere] * 12,
-        out_specs=(in_vmem, in_vmem, in_vmem),
+        out_specs=in_vmem,
         scratch_shapes=[
             pltpu.VMEM((B, COLS, ROWS), jnp.int32),
             pltpu.VMEM((3, OWN, B), f32),
             pltpu.VMEM((3, OWN, B), f32),
             pltpu.VMEM((OWN, B), jnp.int32),
             pltpu.VMEM((ROWS, 384), bf16),
-            pltpu.VMEM((1, 384), f32),
+            pltpu.VMEM((384,), f32),
             pltpu.VMEM((384, 128), bf16),
             pltpu.VMEM((1, 128), f32),
             pltpu.VMEM((128, 128), bf16),
@@ -387,26 +468,29 @@
             pltpu.VMEM((2, ROWS, 128), f32),
             pltpu.VMEM((4, 2, OWN, 128), f32),
             pltpu.VMEM((2, COLS, 128), f32),
-            pltpu.VMEM((256, HALF), f32),
+            pltpu.VMEM((512, 2048), bf16),
+            pltpu.VMEM((2 * COLS, 2048), bf16),
+            pltpu.VMEM((2, 3, 3, 8 * PITCH, 128), f32),
+            pltpu.VMEM((8, 2, COLS, HALF), f32),
             pltpu.VMEM((BINS, ROWS), f32),
             pltpu.VMEM((48, 128), f32),
             pltpu.VMEM((1, ROWS), f32),
-            pltpu.VMEM((128, HALF), f32),
+            pltpu.VMEM((3, 128, 128), f32),
             pltpu.VMEM((32, 16, 128), f32),
             pltpu.VMEM((32, 16, 128), f32),
             pltpu.VMEM((1, 128), f32),
             pltpu.VMEM((128, 1, 128), f32),
             dma((3,)), dma((8,)), dma((8,)), dma((4,)), dma((4,)), dma((4,)), dma((4,)), dma((16,)), dma((32,)), dma((2,)), dma((2,)),
-            dma, dma, dma, dma,
+            dma, dma, dma, dma, pltpu.SemaphoreType.REGULAR,
         ],
-        compiler_params=pltpu.CompilerParams(collective_id=0, has_side_effects=True, vmem_limit_bytes=48 * 1024 * 1024),
+        compiler_params=pltpu.CompilerParams(collective_id=0, has_side_effects=True, vmem_limit_bytes=67043328),
     )(
         neighbor,
         jnp.transpose(true_coords, (1, 2, 0)),
         jnp.transpose(pred_coords, (1, 2, 0)),
         residue_mask.T,
         single.reshape(ROWS, 384),
-        ln_gain.reshape(1, 384),
+        ln_gain,
         w_hidden,
         b_hidden.reshape(1, 128),
         w_mid,
@@ -414,6 +498,12 @@
         w_logits.T,
         b_logits.reshape(1, BINS),
     )
+    score, loss, total = pl.pallas_call(
+        finish,
+        out_shape=(jax.ShapeDtypeStruct((OWN, B), f32), jax.ShapeDtypeStruct((OWN, B), f32), jax.ShapeDtypeStruct((1, 1), f32)),
+        in_specs=[in_vmem],
+        out_specs=(in_vmem, in_vmem, in_vmem),
+    )(out)
     return score.T, loss.T, total.reshape(())
 
 

time: 70.6 us -> 45.4 us (0.64)
  Pallas kernels: 58.1 us -> 44.5 us
  local copies, waits for them, and re-layouts: 9.52 us -> 0 us
  between operations: 2.41 us -> 0.64 us
    pallas_call x1 -> x2, Pallas kernels: 58.1 us -> 44.5 us  [the longest x1 43.2 us: local(): pl.pallas_call(kernel, out_shape=jax.ShapeDtypeStruct((3, OWN, B), f32),...]
    unnamed x22 -> x0, local copies, waits for them, and re-layouts: 8.83 us -> none
where the time goes in v2:
time: 45.4 us; the launch traced here: 45.2 us
  Pallas kernels  44.5 us (98%)
  between operations  0.64 us (1%)
    pallas_call x1, Pallas kernels, local(): pl.pallas_call(kernel, out_shape=jax.ShapeDtypeStruct((3, OWN, B), f32),...  43.2 us
    pallas_call x1, Pallas kernels, local(): pl.pallas_call(finish, out_shape=(jax.ShapeDtypeStruct((OWN, B), f32), ja...  1.38 us

profile of v2, /device:TPU:1, one launch (start us, length us, event | category | flops | bytes accessed | tf_op | source)
XLA Modules:
  0.0 45.2 jit_solution(741181964652815843)
XLA Ops:
  0.6 43.2 %shard_map.139.out = f32[3,24,32]{2,1,0:T(8,128)} custom-call(s32[32,96,768]{2,1,0:T(8,128)} %n_hbm.1, f32[3,24,32]{2,1,0:T(8,128)} %bitcast.12, f32[3,24,32]{2,1,0:T(8,128)} %bitcast.13, s32[24,32]{1,0:T(8,128)} %bitcast.15, bf16[768,384]{1,0:T(8,128)(2,1)} %bitcast.11, f32[384]{0:T(512)} %gain_hbm.1, bf16[384,128]{1,0:T(8,128)(2,1)} %wh_hbm.1, ...), custom_call_target="tpu_custom_call" | custom-call | tf_op jit(solution)/shard_map/pallas_call | solution.py:449
  43.8 1.4 %shard_map.140 = (f32[24,32]{1,0:T(8,128)}, f32[24,32]{1,0:T(8,128)}, f32[1,1]{1,0:T(1,128)}) custom-call(f32[3,24,32]{2,1,0:T(8,128)} %shard_map.139.out), custom_call_target="tpu_custom_call" | custom-call | tf_op jit(solution)/shard_map/pallas_call | solution.py:501

commit v3 on v2

--- a/solution.py
+++ b/solution.py
@@ -15,7 +15,7 @@
 HALF = 384
 BINS = 50
 MESH = pl.DeviceIdType.MESH
-SPLIT = 3
+SPLIT = 5
 PITCH = 33
 
 
@@ -27,7 +27,7 @@
     n_hbm, tc_hbm, pc_hbm, mask_hbm, single_hbm, gain_hbm, wh_hbm, bh_hbm, wm_hbm, bm_hbm, wl_hbm, bl_hbm,
     out,
     nbuf, tc, pc, mask, single, gain, wh, bh, wm, bm, wl, bl,
-    blk, rows, zbuf, colbuf, pick_left, left, right, dist, logits, stats, logz, pr, rs_send, rs_recv, ar_send, ar_buf,
+    blk, rblk, rows, zbuf, colbuf, pick_left, left, right, dist, logits, stats, logz, pr, rs_send, rs_recv, ar_send, ar_buf,
     in_sem, n_sem, w_sem, z_ssem, z_rsem, c_ssem, c_rsem, g_ssem, g_rsem, f_ssem, f_rsem,
     rs_ssem, rs_rsem, ar_ssem, ar_rsem, far_in,
 ):
@@ -75,8 +75,15 @@
         blk[1, :, i * 32 : (i + 1) * 32] = pc[i] * 2.0
     blk[0, :, 96:128] = valid
     blk[1, :, 96:128] = valid
-    own_rows = pl.ds(pl.multiple_of(c * OWN, 8), OWN)
-    rows[:, own_rows, :] = blk[...]
+    for i, part in enumerate((tc[0], tc[1], tc[2], pc[0])):
+        rblk[0:24, i * 32 : (i + 1) * 32] = part * 2.0
+    for i in range(3):
+        at = slice(24 + 8 * (i // 2), 32 + 8 * (i // 2))
+        for j in range(2):
+            lo = (i % 2) * 64 + j * 32
+            rblk[at, lo : lo + 32] = pc[1 + j, 8 * i : 8 * i + 8, :] * 2.0
+    rblk[32:40, 64:128] = jnp.zeros((8, 64), jnp.float32)
+    rows[c] = rblk[...]
     pl.semaphore_wait(barrier, 19)
     pl.semaphore_signal(far_in, inc=1, device_id=(z, mirror), device_id_type=MESH)
 
@@ -113,7 +120,7 @@
         xx = jnp.where(d < 8, half, other) * 2 + lax.rem(x + lax.rem(lax.div(d, 4), 2), 2)
         to = plane(xx, lax.rem(y + lax.rem(d, 4), 4), k)
         return pltpu.make_async_remote_copy(
-            blk, rows.at[:, own_rows, :], g_ssem.at[d], g_rsem.at[c], device_id=(z, to), device_id_type=MESH
+            rblk, rows.at[c], g_ssem.at[d], g_rsem.at[c], device_id=(z, to), device_id_type=MESH
         )
 
     def row_source(d):
@@ -121,20 +128,18 @@
         return plane(xx, lax.rem(y + lax.rem(d, 4), 4), k)
 
     def forward(src_c, d):
-        at = pl.ds(pl.multiple_of(src_c * OWN, 8), OWN)
         sem = 0 if d < 8 else 1
         return pltpu.make_async_remote_copy(
-            rows.at[:, at, :], rows.at[:, at, :], f_ssem.at[sem], f_rsem.at[sem], device_id=(z, partner), device_id_type=MESH
+            rows.at[src_c], rows.at[src_c], f_ssem.at[sem], f_rsem.at[sem], device_id=(z, partner), device_id_type=MESH
         )
 
     def row_arrival(src_c, d):
-        at = pl.ds(pl.multiple_of(src_c * OWN, 8), OWN)
         pltpu.make_async_remote_copy(
-            rows.at[:, at, :], rows.at[:, at, :], g_ssem.at[d], g_rsem.at[src_c], device_id=(z, partner), device_id_type=MESH
+            rows.at[src_c], rows.at[src_c], g_ssem.at[d], g_rsem.at[src_c], device_id=(z, partner), device_id_type=MESH
         ).wait_recv()
 
     pltpu.make_async_remote_copy(
-        blk, rows.at[:, own_rows, :], f_ssem.at[0], f_rsem.at[0], device_id=(z, partner), device_id_type=MESH
+        rblk, rows.at[c], f_ssem.at[0], f_rsem.at[0], device_id=(z, partner), device_id_type=MESH
     ).start()
     for d in range(1, 8):
         row_copy(d).start()
@@ -143,28 +148,6 @@
     col_start(blk, 0)
     for d in range(8, 16):
         row_copy(d).start()
-    for s in head:
-        s.wait()
-    feats = single[...].astype(jnp.float32)
-    average = jnp.sum(feats, axis=-1, keepdims=True) * (1.0 / 384)
-    centred = feats - average
-    variance = jnp.sum(centred * centred, axis=-1, keepdims=True) * (1.0 / 384)
-    normed = (centred * lax.rsqrt(variance + 1e-05) * gain[...].reshape(1, 384)).astype(jnp.bfloat16)
-    first = jnp.maximum(jnp.dot(normed, wh[...], preferred_element_type=jnp.float32) + bh[...], 0.0).astype(jnp.bfloat16)
-    second = jnp.maximum(jnp.dot(first, wm[...], preferred_element_type=jnp.float32) + bm[...], 0.0).astype(jnp.bfloat16)
-    for g in range(6):
-        at = lax.broadcasted_iota(jnp.int32, (1, 128), 1) + g * 128
-        source = lax.bitwise_and(at, 31) * OWN + lax.shift_right_logical(at, 5)
-        pick = (lax.broadcasted_iota(jnp.int32, (ROWS, 128), 0) == source).astype(jnp.float32).astype(jnp.bfloat16)
-        moved = lax.dot_general(second, pick, (((0,), (0,)), ((), ())), preferred_element_type=jnp.float32)
-        logits[:, g * 128 : (g + 1) * 128] = jnp.dot(wl[...], moved.astype(jnp.bfloat16), preferred_element_type=jnp.float32)
-    eye = lax.broadcasted_iota(jnp.int32, (BINS, BINS), 0) == lax.broadcasted_iota(jnp.int32, (BINS, BINS), 1)
-    bias = jnp.sum(jnp.where(eye, bl[...], 0.0), axis=1, keepdims=True)
-    with_bias = logits[...] + bias
-    logits[...] = with_bias
-    top = jnp.max(with_bias, axis=0, keepdims=True)
-    logz[...] = top + jnp.log(jnp.sum(jnp.exp(with_bias - top), axis=0, keepdims=True))
-
     for i in range(16):
         at = lax.broadcasted_iota(jnp.int32, (1, 128), 1) + i * 128
         b_of = lax.shift_right_logical(at, 6)
@@ -189,7 +172,7 @@
 
     def forwards_done(sem):
         pltpu.make_async_remote_copy(
-            rows.at[:, pl.ds(0, 8 * OWN), :], rows.at[:, pl.ds(0, 8 * OWN), :], f_ssem.at[sem], f_rsem.at[sem],
+            rows.at[pl.ds(0, 8)], rows.at[pl.ds(0, 8)], f_ssem.at[sem], f_rsem.at[sem],
             device_id=(z, partner), device_id_type=MESH,
         ).wait_recv()
 
@@ -226,16 +209,24 @@
         both = jnp.concatenate(both, axis=0)
         for i in range(8):
             at = slice(i * 256, (i + 1) * 256)
-            left[:, at] = jnp.dot(both, pick_left[:, at], preferred_element_type=jnp.float32).astype(jnp.bfloat16)
+            full = jnp.dot(both, pick_left[:, at], preferred_element_type=jnp.float32)
+            even = lax.rem(lax.broadcasted_iota(jnp.int32, (1, 256), 1), 128) < 64
+            left[0, :, at] = jnp.where(even, full, 0.0).astype(jnp.bfloat16)
+            left[1, :, at] = jnp.where(even, 0.0, full).astype(jnp.bfloat16)
 
     def turn(h):
         one = jnp.full((32, 128), 1.0, jnp.float32)
+        shifted = pltpu.roll(colbuf[1, 0:1, :], 96, 1)
+        some = pl.ds(h * 16, 16)
+        wide = rows[some, 0:24, :].reshape(HALF, 128) - jnp.where(lane < 96, colbuf[0, 0:1, :], shifted)
+        u = rows[some, 24:32, :]
+        rest = jnp.concatenate([u, pltpu.roll(u, 64, 2), rows[some, 32:40, :]], axis=1).reshape(HALF, 128) - shifted
+        flats = [
+            (jnp.transpose(wide[v * 128 : (v + 1) * 128]), jnp.transpose(rest[v * 128 : (v + 1) * 128])) for v in range(3)
+        ]
         for t in range(2):
-            mid = centre(t)
             for v in range(3):
-                at = pl.ds(pl.multiple_of(h * HALF + v * 128, 128), 128)
-                flat = jnp.transpose(rows[t, at, :] - mid)
-                xyz = flat[0:96]
+                xyz = flats[v][0][0:96] if t == 0 else jnp.concatenate([flats[v][0][96:128], flats[v][1][0:64]], axis=0)
                 sq = xyz * xyz
                 m = pieces((sq[0:32] + sq[32:64]) + (sq[64:96] + 4e-10))
                 p = pieces(xyz * -2.0)
@@ -243,20 +234,21 @@
                     for slot, rows32 in enumerate((p[q][0:32], p[q][32:64], p[q][64:96], u) + (p[q][0:32], p[q][32:64], p[q][64:96], w)):
                         right[t, q, v, slot * PITCH : slot * PITCH + 32, :] = rows32
 
-    def distances(b, i, s, dst):
+    def distances(i, dst0, dst1):
         at = pl.ds(pl.multiple_of(i * 128, 128), 128)
+        gap = jnp.zeros((16, 128), jnp.float32)
         for t in range(2):
-            lhs = left[t * COLS : (t + 1) * COLS, at]
+            lhs = jnp.concatenate([left[0, t * COLS : (t + 1) * COLS, at], left[1, t * COLS : (t + 1) * COLS, at]], axis=0)
             cols = []
             for v in range(3):
-                vs = [right[t, q, v, pl.ds(b, 8, stride=PITCH), :] for q in range(3)]
-                cols.append(jnp.concatenate([vs[0], vs[0], vs[1], vs[1], vs[2], vs[2]], axis=0).astype(jnp.bfloat16))
-            rhs = jnp.concatenate(cols, axis=1)
-            if s == 0:
-                rhs = jnp.concatenate([rhs, jnp.zeros((80, HALF), jnp.bfloat16)], axis=0)
-            else:
-                rhs = jnp.concatenate([jnp.zeros((64, HALF), jnp.bfloat16), rhs, jnp.zeros((16, HALF), jnp.bfloat16)], axis=0)
-            dst[t] = jnp.dot(lhs, rhs, preferred_element_type=jnp.float32)
+                tall = []
+                for s in range(2):
+                    vs = [right[t, q, v, pl.ds(2 * i + s, 8, stride=PITCH), :] for q in range(3)]
+                    tall += [vs[0], vs[0], vs[1], vs[1], vs[2], vs[2], gap]
+                cols.append(jnp.concatenate(tall, axis=0).astype(jnp.bfloat16))
+            both = jnp.dot(lhs, jnp.concatenate(cols, axis=1), preferred_element_type=jnp.float32)
+            dst0[t] = both[:COLS]
+            dst1[t] = both[COLS:]
 
     def pairs(h):
         def one(b, src):
@@ -288,8 +280,8 @@
             def quad(now, later):
                 for j in range(4):
                     one(4 * i + j, dist.at[now + j])
-                for j in range(4):
-                    distances(4 * after + j, 2 * after + j // 2, j % 2, dist.at[later + j])
+                for j in range(2):
+                    distances(2 * after + j, dist.at[later + 2 * j], dist.at[later + 2 * j + 1])
 
             @pl.when(lax.rem(i, 2) == 0)
             def _():
@@ -331,8 +323,8 @@
 
     left_sides()
     turn(half)
-    for j in range(4):
-        distances(j, j // 2, j % 2, dist.at[j])
+    for j in range(2):
+        distances(j, dist.at[2 * j], dist.at[2 * j + 1])
     lax.fori_loop(0, SPLIT, pairs(half), 0)
     for d in range(8, 16):
         src_c = row_source(d)
@@ -342,10 +334,32 @@
     share(half)
     forwards_done(1)
     turn(other)
-    for j in range(4):
-        distances(j, j // 2, j % 2, dist.at[j])
+    for j in range(2):
+        distances(j, dist.at[2 * j], dist.at[2 * j + 1])
     lax.fori_loop(0, B // 4, pairs(other), 0)
     share(other)
+
+    for s in head:
+        s.wait()
+    feats = single[...].astype(jnp.float32)
+    average = jnp.sum(feats, axis=-1, keepdims=True) * (1.0 / 384)
+    centred = feats - average
+    variance = jnp.sum(centred * centred, axis=-1, keepdims=True) * (1.0 / 384)
+    normed = (centred * lax.rsqrt(variance + 1e-05) * gain[...].reshape(1, 384)).astype(jnp.bfloat16)
+    first = jnp.maximum(jnp.dot(normed, wh[...], preferred_element_type=jnp.float32) + bh[...], 0.0).astype(jnp.bfloat16)
+    second = jnp.maximum(jnp.dot(first, wm[...], preferred_element_type=jnp.float32) + bm[...], 0.0).astype(jnp.bfloat16)
+    for g in range(6):
+        at = lax.broadcasted_iota(jnp.int32, (1, 128), 1) + g * 128
+        source = lax.bitwise_and(at, 31) * OWN + lax.shift_right_logical(at, 5)
+        pick = (lax.broadcasted_iota(jnp.int32, (ROWS, 128), 0) == source).astype(jnp.float32).astype(jnp.bfloat16)
+        moved = lax.dot_general(second, pick, (((0,), (0,)), ((), ())), preferred_element_type=jnp.float32)
+        logits[:, g * 128 : (g + 1) * 128] = jnp.dot(wl[...], moved.astype(jnp.bfloat16), preferred_element_type=jnp.float32)
+    eye = lax.broadcasted_iota(jnp.int32, (BINS, BINS), 0) == lax.broadcasted_iota(jnp.int32, (BINS, BINS), 1)
+    bias = jnp.sum(jnp.where(eye, bl[...], 0.0), axis=1, keepdims=True)
+    with_bias = logits[...] + bias
+    logits[...] = with_bias
+    top = jnp.max(with_bias, axis=0, keepdims=True)
+    logz[...] = top + jnp.log(jnp.sum(jnp.exp(with_bias - top), axis=0, keepdims=True))
 
     everyone = lambda a, b: pltpu.make_async_remote_copy(
         rs_send.at[pl.ds(0, 31)], rs_recv.at[pl.ds(0, 31)], rs_ssem, rs_rsem, device_id=(z, partner), device_id_type=MESH
@@ -420,7 +434,7 @@
         row_copy(d).wait_send()
     for sem in range(2):
         pltpu.make_async_remote_copy(
-            rows.at[:, pl.ds(0, 8 * OWN), :], rows.at[:, pl.ds(0, 8 * OWN), :], f_ssem.at[sem], f_rsem.at[sem],
+            rows.at[pl.ds(0, 8)], rows.at[pl.ds(0, 8)], f_ssem.at[sem], f_rsem.at[sem],
             device_id=(z, partner), device_id_type=MESH,
         ).wait_send()
     everyone(0, 0).wait_send()
@@ -465,11 +479,12 @@
             pltpu.VMEM((BINS, 128), bf16),
             pltpu.VMEM((1, BINS), f32),
             pltpu.VMEM((2, OWN, 128), f32),
-            pltpu.VMEM((2, ROWS, 128), f32),
+            pltpu.VMEM((40, 128), f32),
+            pltpu.VMEM((32, 40, 128), f32),
             pltpu.VMEM((4, 2, OWN, 128), f32),
             pltpu.VMEM((2, COLS, 128), f32),
             pltpu.VMEM((512, 2048), bf16),
-            pltpu.VMEM((2 * COLS, 2048), bf16),
+            pltpu.VMEM((2, 2 * COLS, 2048), bf16),
             pltpu.VMEM((2, 3, 3, 8 * PITCH, 128), f32),
             pltpu.VMEM((8, 2, COLS, HALF), f32),
             pltpu.VMEM((BINS, ROWS), f32),

time: 45.4 us -> 44.8 us (0.987)
  Pallas kernels: 44.5 us -> 44 us
    pallas_call x1, Pallas kernels: 43.2 us -> 42.6 us  [local(): pl.pallas_call(kernel, out_shape=jax.ShapeDtypeStruct((3, OWN, B), f32),...]
where the time goes in v3:
time: 44.8 us; the launch traced here: 44.7 us
  Pallas kernels  44 us (98%)
  between operations  0.64 us (1%)
    pallas_call x1, Pallas kernels, local(): pl.pallas_call(kernel, out_shape=jax.ShapeDtypeStruct((3, OWN, B), f32),...  42.6 us
    pallas_call x1, Pallas kernels, local(): pl.pallas_call(finish, out_shape=(jax.ShapeDtypeStruct((OWN, B), f32), ja...  1.38 us

profile of v3, /device:TPU:1, one launch (start us, length us, event | category | flops | bytes accessed | tf_op | source)
XLA Modules:
  0.0 44.7 jit_solution(10712899153785745364)
XLA Ops:
  0.6 42.6 %shard_map.139.out = f32[3,24,32]{2,1,0:T(8,128)} custom-call(s32[32,96,768]{2,1,0:T(8,128)} %n_hbm.1, f32[3,24,32]{2,1,0:T(8,128)} %bitcast.12, f32[3,24,32]{2,1,0:T(8,128)} %bitcast.13, s32[24,32]{1,0:T(8,128)} %bitcast.15, bf16[768,384]{1,0:T(8,128)(2,1)} %bitcast.11, f32[384]{0:T(512)} %gain_hbm.1, bf16[384,128]{1,0:T(8,128)(2,1)} %wh_hbm.1, ...), custom_call_target="tpu_custom_call" | custom-call | tf_op jit(solution)/shard_map/pallas_call | solution.py:463
  43.3 1.4 %shard_map.140 = (f32[24,32]{1,0:T(8,128)}, f32[24,32]{1,0:T(8,128)}, f32[1,1]{1,0:T(1,128)}) custom-call(f32[3,24,32]{2,1,0:T(8,128)} %shard_map.139.out), custom_call_target="tpu_custom_call" | custom-call | tf_op jit(solution)/shard_map/pallas_call | solution.py:516
